TPU v7x, 32 devices: a whole 2x2x4 slice. The times are simulated.
32 devices in a mesh: group: 4 (over y, x), shard: 8 (over z, core).
Axes of the slice: x: 2, y: 2, z: 4, core: 2. Of those that a mesh axis runs over, the one named last changes fastest.
Arguments:
- embeddings: bfloat16 [128, 256, 768], P(('group', 'shard')), may hold values from -6 to 6
- assignments: int32 [128, 2, 256], P(('group', 'shard')), may hold values from 0 to 4095, as said below
- block_group: int32 [128], P(('group', 'shard')), may hold values from 0 to 3, as said below
- centroids: float32 [4, 4096, 768], P('group'), may hold values from -6 to 6
Outputs:
- subcentroids: float32 [4, 4096, 768], P('group', 'shard')
- inertia: float32 [4, 4096], P('group', 'shard')
Inputs may be any that keep to these rules, and one draw needn't show every extreme that they name: `block_group`: of the 4 blocks of one device at most 2 name the same group; in every draw, for some group and some shard index, every device of that shard index has exactly 2 blocks naming that group. `assignments`: labels k with the same k // 512 form one range. In each block and iteration at most 64 rows have labels in one range; in every draw there is an iteration in which every block has exactly 64 rows in one common range.
All inputs are finite; a program needn't handle non-finite values.
Results may differ from a plain program's by a relative error of at most 0.0003.
Values may be sent and summed in bfloat16 or wider, within the bound.
A program may use at most 128 MiB of HBM per device.

v0:
```python
import functools

import jax
import jax.numpy as jnp
from jax import lax
from jax.experimental import pallas as pl
from jax.experimental.pallas import tpu as pltpu
from jax.sharding import PartitionSpec as P

PRIOR = 8.0
META = 8
CHUNKS = 3
MESH = pl.DeviceIdType.MESH


def exchange_kernel(n_gather, n_swap, width, column, *refs):
    n_in = n_gather + n_swap
    gathers, swaps = refs[:n_gather], refs[n_gather:n_in]
    outs = refs[n_in : 2 * n_in]
    gather_outs, swap_outs = outs[:n_gather], outs[n_gather:]
    scratch = refs[2 * n_in :]
    stages = scratch[:n_gather]
    scratch = scratch[n_gather:]

    groups, shards = lax.axis_size("group"), lax.axis_size("shard")
    chips = shards // 2
    mine, place = lax.axis_index("group"), lax.axis_index("shard")
    chip, core = place // 2, place % 2
    partner = (mine, chip * 2 + 1 - core)
    right = (mine, lax.rem(chip + 1, chips) * 2 + core)
    left = (mine, lax.rem(chip + chips - 1, chips) * 2 + core)

    def peer(step):
        return lax.rem(mine + step, groups)

    barrier = pltpu.get_barrier_semaphore()
    greeted = 0
    if n_gather:
        for device in (left, right, partner):
            pl.semaphore_signal(barrier, inc=1, device_id=device, device_id_type=MESH)
        greeted += 3
    if n_swap:
        for step in range(1, groups):
            pl.semaphore_signal(
                barrier, inc=1, device_id=(peer(step), place), device_id_type=MESH
            )
        greeted += groups - 1

    loads = []
    if n_gather:
        load_sem = scratch[0]
        for i in range(n_gather):
            source = gathers[i]
            if i == 0:
                source = source.at[:, :, pl.ds(column, width)]
            load = pltpu.make_async_copy(source, stages[i], load_sem.at[i])
            load.start()
            loads.append(load)
    pl.semaphore_wait(barrier, greeted)

    swap_copies = []
    if n_swap:
        swap_send, swap_recv = scratch[-2:]
        for step in range(1, groups):
            for i in range(n_swap):
                copy = pltpu.make_async_remote_copy(
                    src_ref=swaps[i].at[peer(step)],
                    dst_ref=swap_outs[i].at[step - 1],
                    send_sem=swap_send.at[i, step - 1],
                    recv_sem=swap_recv.at[i, step - 1],
                    device_id=(peer(step), place),
                    device_id_type=MESH,
                )
                copy.start()
                swap_copies.append(copy)

    if n_gather:
        store_sem, send_r, recv_r, send_l, recv_l, send_p, recv_p = scratch[1:8]
        stores = []

        def hop(i, source, origin, step, to, sends, recvs):
            return pltpu.make_async_remote_copy(
                src_ref=source,
                dst_ref=gather_outs[i].at[origin * 2 + core],
                send_sem=sends.at[i, step],
                recv_sem=recvs.at[i, step],
                device_id=to,
                device_id_type=MESH,
            )

        for i in range(n_gather):
            loads[i].wait()
            store = pltpu.make_async_copy(
                stages[i], gather_outs[i].at[place], store_sem.at[i]
            )

            @pl.when(chip < chips - 1)
            def _():
                hop(i, stages[i], chip, 0, right, send_r, recv_r).start()

            @pl.when(chip > 0)
            def _():
                hop(i, stages[i], chip, 0, left, send_l, recv_l).start()

            hop(i, stages[i], chip, chip, partner, send_p, recv_p).start()
            store.start()
            stores.append(store)

        for step in range(chips - 1):
            for i in range(n_gather):
                from_left = chip - 1 - step

                @pl.when(from_left >= 0)
                def _():
                    block = gather_outs[i].at[from_left * 2 + core]
                    hop(i, block, from_left, step, right, send_r, recv_r).wait_recv()

                    if step < chips - 2:

                        @pl.when(chip < chips - 1)
                        def _():
                            hop(i, block, from_left, step + 1, right, send_r, recv_r).start()

                    hop(i, block, from_left, from_left, partner, send_p, recv_p).start()

                from_right = chip + 1 + step

                @pl.when(from_right <= chips - 1)
                def _():
                    block = gather_outs[i].at[from_right * 2 + core]
                    hop(i, block, from_right, step, left, send_l, recv_l).wait_recv()

                    if step < chips - 2:

                        @pl.when(chip > 0)
                        def _():
                            hop(i, block, from_right, step + 1, left, send_l, recv_l).start()

                    hop(i, block, from_right, from_right, partner, send_p, recv_p).start()

        for i in range(n_gather):
            stores[i].wait()
            for step in range(chips - 1):

                @pl.when((chip - step >= 0) & (chip < chips - 1))
                def _():
                    hop(i, stages[i], chip, step, right, send_r, recv_r).wait_send()

                @pl.when((chip + step <= chips - 1) & (chip > 0))
                def _():
                    hop(i, stages[i], chip, step, left, send_l, recv_l).wait_send()

            for origin in range(chips):
                hop(i, stages[i], origin, origin, partner, send_p, recv_p).wait()

    for copy in swap_copies:
        copy.wait()


def exchange(gathers, swaps, width, column, key):
    groups, shards = lax.axis_size("group"), lax.axis_size("shard")
    chips = shards // 2
    n_gather, n_swap = len(gathers), len(swaps)
    shapes, scratch = [], []
    for i, array in enumerate(gathers):
        block = array.shape[:-1] + (width if i == 0 else array.shape[-1],)
        shapes.append(jax.ShapeDtypeStruct((shards,) + block, array.dtype))
        scratch.append(pltpu.VMEM(block, array.dtype))
    for array in swaps:
        shapes.append(jax.ShapeDtypeStruct((groups - 1,) + array.shape[1:], array.dtype))
    dma = pltpu.SemaphoreType.DMA
    if n_gather:
        scratch += [dma((n_gather,)), dma((n_gather,))]
        scratch += [dma((n_gather, max(chips - 1, 1)))] * 4
        scratch += [dma((n_gather, chips))] * 2
    if n_swap:
        scratch += [dma((n_swap, groups - 1))] * 2
    return pl.pallas_call(
        functools.partial(exchange_kernel, n_gather, n_swap, width, column),
        out_shape=shapes,
        in_specs=[pl.BlockSpec(memory_space=pl.ANY)] * (n_gather + n_swap),
        out_specs=[pl.BlockSpec(memory_space=pl.ANY)] * (n_gather + n_swap),
        scratch_shapes=scratch,
        compiler_params=pltpu.CompilerParams(collective_id=key, has_side_effects=True),
    )(*gathers, *swaps)


def tally_kernel(per_step, iters, with_extra, owners, labels, extra, rows, sums, *more):
    step = pl.program_id(0)
    centers = sums.shape[2]
    block_rows = rows.shape[1]

    @pl.when(step == 0)
    def _():
        sums[...] = jnp.zeros_like(sums)
        if with_extra:
            more[0][...] = jnp.zeros_like(more[0])

    ids = lax.broadcasted_iota(jnp.int32, (centers, block_rows), 0)
    for block in range(per_step):
        owner = owners[step * per_step + block]
        for t in range(iters):
            onehot = (ids == labels[block, t : t + 1, :]).astype(jnp.bfloat16)
            sums[owner, t] += jnp.dot(
                onehot, rows[block], preferred_element_type=jnp.float32
            )
            if with_extra:
                more[0][owner, t] += lax.dot_general(
                    extra[block],
                    onehot,
                    (((1,), (1,)), ((), ())),
                    preferred_element_type=jnp.float32,
                )


def tally(owners, labels, extra, rows, groups, centers, per_step, with_extra):
    blocks, iters, block_rows = labels.shape
    width = rows.shape[-1]
    shapes = [jax.ShapeDtypeStruct((groups, iters, centers, width), jnp.float32)]
    if with_extra:
        shapes.append(jax.ShapeDtypeStruct((groups, iters, extra.shape[1], centers), jnp.float32))
    out_specs = [pl.BlockSpec(s.shape, lambda i, o: (0, 0, 0, 0)) for s in shapes]
    return pl.pallas_call(
        functools.partial(tally_kernel, per_step, iters, with_extra),
        out_shape=shapes,
        grid_spec=pltpu.PrefetchScalarGridSpec(
            num_scalar_prefetch=1,
            grid=(blocks // per_step,),
            in_specs=[
                pl.BlockSpec((per_step, iters, block_rows), lambda i, o: (i, 0, 0)),
                pl.BlockSpec((per_step,) + extra.shape[1:], lambda i, o: (i, 0, 0)),
                pl.BlockSpec((per_step, block_rows, width), lambda i, o: (i, 0, 0)),
            ],
            out_specs=out_specs,
        ),
        compiler_params=pltpu.CompilerParams(vmem_limit_bytes=48 * 2**20),
    )(owners, labels, extra, rows)


def body(embeddings, assignments, block_group, centroids):
    groups, shards = lax.axis_size("group"), lax.axis_size("shard")
    mine, place = lax.axis_index("group"), lax.axis_index("shard")
    local, block_rows, features = embeddings.shape
    iters = assignments.shape[1]
    owned = centroids.shape[1] // shards
    chunks = CHUNKS if features % (CHUNKS * 128) == 0 else 1
    width = features // chunks
    blocks = shards * local

    wide = embeddings.astype(jnp.float32)
    squares = jnp.sum(wide * wide, axis=2)
    meta = jnp.concatenate(
        [
            assignments.astype(jnp.float32),
            jnp.broadcast_to(
                block_group[:, None, None].astype(jnp.float32), (local, 1, block_rows)
            ),
            squares[:, None, :],
            jnp.zeros((local, META - iters - 2, block_rows), jnp.float32),
        ],
        axis=1,
    )

    rows, metas = exchange([embeddings, meta], [], width, 0, 0)
    metas = metas.reshape(blocks, META, block_rows)
    labels = metas[:, :iters].astype(jnp.int32) - place * owned
    owners = metas[:, iters, 0].astype(jnp.int32)
    square = metas[:, iters + 1]
    high = lax.reduce_precision(square, 8, 7)
    middle = lax.reduce_precision(square - high, 8, 7)
    low = square - high - middle
    one = jnp.ones_like(square)
    zero = jnp.zeros_like(square)
    extra = jnp.stack([one, high, middle, low] + [zero] * 12, axis=1).astype(jnp.bfloat16)

    totals = []
    tail = None
    pending = []
    for chunk in range(chunks):
        result = tally(
            owners,
            labels,
            extra,
            rows.reshape(blocks, block_rows, width),
            groups,
            owned,
            local,
            chunk == 0,
        )
        column = (chunk + 1) * width
        if chunk + 1 < chunks:
            rows, *got = exchange([embeddings], result, width, column, chunk + 1)
        else:
            got = exchange([], result, width, 0, chunk + 1)
        whole = [
            lax.dynamic_index_in_dim(kept, mine, 0, keepdims=False) + jnp.sum(came, axis=0)
            for kept, came in zip(result, got)
        ]
        totals.append(whole[0])
        if chunk == 0:
            tail = whole[1]

    prior = lax.dynamic_slice_in_dim(centroids[0], place * owned, owned, 0)
    counts = tail[:, 0]
    within = tail[iters - 1, 1] + tail[iters - 1, 2] + tail[iters - 1, 3]
    pieces = []
    for chunk in range(chunks):
        previous = prior[:, chunk * width : (chunk + 1) * width]
        for t in range(iters):
            sums = totals[chunk][t]
            count = counts[t][:, None]
            if t == iters - 1:
                within = within + jnp.sum(
                    previous * (count * previous - 2.0 * sums), axis=1
                )
            previous = (sums + PRIOR * previous) / (count + PRIOR)
        pieces.append(previous)
    inertia = within / ((counts[iters - 1] + PRIOR) * features)
    return (jnp.concatenate(pieces, axis=1)[None], inertia[None])


def solution(mesh):
    in_specs = (
        P(("group", "shard"), None, None),
        P(("group", "shard"), None, None),
        P(("group", "shard")),
        P("group", None, None),
    )
    out_specs = (P("group", "shard", None), P("group", "shard"))
    return jax.shard_map(body, mesh=mesh, in_specs=in_specs, out_specs=out_specs, check_vma=False)
```

profile of v0, /device:TPU:0, one launch (start us, length us, event | category | flops | bytes accessed | tf_op | source)
XLA Modules:
  0.0 258.1 jit_solution(8858427478289250125)
XLA Ops:
  0.6 0.7 convert_element_type.20
  1.3 0.1 pad.6.clone
  1.4 0.1 broadcast_in_dim.16
  1.4 1.8 multiply_reduce_fusion
  3.2 0.7 convert_element_type.19
  4.0 0.7 maximum_maximum_fusion.refs_1_
  4.6 1.5 dynamic-slice_bitcast_fusion
  6.1 44.9 %shard_map.59 = (bf16[8,4,256,256]{3,2,1,0:T(8,128)(2,1)}, f32[8,4,8,256]{3,2,1,0:T(8,128)}) custom-call(bf16[4,256,768]{2,1,0:T(8,128)(2,1)} %refs_0_.5, f32[4,8,256]{2,1,0:T(8,128)} %maximum_maximum_fusion.refs_1_), custom_call_target="tpu_custom_call" | custom-call | tf_op jit(solution)/shard_map/pallas_call | solution.py:178
  51.0 1.6 fusion.8.owners
  52.6 1.0 fusion.6.labels
  53.6 1.0 fusion.7
  54.7 0.2 stack.15.extra
  55.0 11.9 %shard_map.60 = (f32[4,2,512,256]{3,2,1,0:T(8,128)S(1)}, f32[4,2,16,512]{3,2,1,0:T(8,128)S(1)}) custom-call(s32[32]{0:T(128)S(1)} %fusion.8.owners, s32[32,2,256]{2,1,0:T(2,128)S(1)} %fusion.6.labels, bf16[32,16,256]{2,1,0:T(8,128)(2,1)S(1)} %stack.15.extra, bf16[32,256,256]{2,1,0:T(8,128)(2,1)} %bitcast.73), custom_call_target="tpu_custom_call" | custom-call | tf_op jit(solution)/shard_map/pallas_call | solution.py:223
  66.9 0.0 copy-start.2
  66.9 1.9 copy-done.2
  68.8 0.0 copy-start.3
  68.8 0.7 copy-done.3
  69.5 52.4 %shard_map.61 = (bf16[8,4,256,256]{3,2,1,0:T(8,128)(2,1)}, f32[3,2,512,256]{3,2,1,0:T(8,128)}, f32[3,2,16,512]{3,2,1,0:T(8,128)}) custom-call(bf16[4,256,768]{2,1,0:T(8,128)(2,1)} %refs_0_.5, f32[4,2,512,256]{3,2,1,0:T(8,128)} %copy-done.2, f32[4,2,16,512]{3,2,1,0:T(8,128)} %copy-done.3), custom_call_target="tpu_custom_call" | custom-call | tf_op jit(solution)/shard_map/pallas_call | solution.py:178
  121.9 0.0 copy-start.4
  121.9 3.2 %reduce_sum.79 = f32[2,512,256]{2,1,0:T(8,128)} reduce(f32[3,2,512,256]{3,2,1,0:T(8,128)} %get-tuple-element.15, f32[]{:T(128)} %constant.14.clone.1), dimensions={0}, to_apply=%region_1.2 | reduce | flops 524288 | bytes 4194308 | tf_op jit(solution)/shard_map/reduce_sum | solution.py:296
  125.1 1.7 bitcast_add_fusion.2
  126.8 0.0 copy-done.4
  126.9 0.9 bitcast_add_fusion.3
  127.7 0.2 add_divide_fusion.2
  128.0 8.7 %shard_map.62.refs_1_ = f32[4,2,512,256]{3,2,1,0:T(8,128)S(1)} custom-call(s32[32]{0:T(128)S(1)} %fusion.8.owners, s32[32,2,256]{2,1,0:T(2,128)S(1)} %fusion.6.labels, bf16[32,16,256]{2,1,0:T(8,128)(2,1)S(1)} %stack.15.extra, bf16[32,256,256]{2,1,0:T(8,128)(2,1)} %bitcast.74), custom_call_target="tpu_custom_call" | custom-call | tf_op jit(solution)/shard_map/pallas_call | solution.py:223
  136.7 0.0 copy-start.1
  136.7 1.9 copy-done.1
  138.6 49.4 %shard_map.63 = (bf16[8,4,256,256]{3,2,1,0:T(8,128)(2,1)}, f32[3,2,512,256]{3,2,1,0:T(8,128)}) custom-call(bf16[4,256,768]{2,1,0:T(8,128)(2,1)} %refs_0_.5, f32[4,2,512,256]{3,2,1,0:T(8,128)} %copy-done.1), custom_call_target="tpu_custom_call" | custom-call | tf_op jit(solution)/shard_map/pallas_call | solution.py:178
  188.0 3.2 %reduce_sum.81 = f32[2,512,256]{2,1,0:T(8,128)} reduce(f32[3,2,512,256]{3,2,1,0:T(8,128)} %get-tuple-element.18, f32[]{:T(128)} %constant.14.clone.1), dimensions={0}, to_apply=%region_3.4 | reduce | flops 524288 | bytes 4194308 | tf_op jit(solution)/shard_map/reduce_sum | solution.py:296
  191.2 8.7 %shard_map.64.refs_0_ = f32[4,2,512,256]{3,2,1,0:T(8,128)S(1)} custom-call(s32[32]{0:T(128)S(1)} %fusion.8.owners, s32[32,2,256]{2,1,0:T(2,128)S(1)} %fusion.6.labels, bf16[32,16,256]{2,1,0:T(8,128)(2,1)S(1)} %stack.15.extra, bf16[32,256,256]{2,1,0:T(8,128)(2,1)} %bitcast.75), custom_call_target="tpu_custom_call" | custom-call | tf_op jit(solution)/shard_map/pallas_call | solution.py:223
  199.9 0.0 copy-start
  199.9 2.0 copy-done
  201.9 47.9 %shard_map.65 = f32[3,2,512,256]{3,2,1,0:T(8,128)} custom-call(f32[4,2,512,256]{3,2,1,0:T(8,128)} %copy-done), custom_call_target="tpu_custom_call" | custom-call | tf_op jit(solution)/shard_map/pallas_call | solution.py:178
  249.8 3.2 %reduce_sum.82 = f32[2,512,256]{2,1,0:T(8,128)} reduce(f32[3,2,512,256]{3,2,1,0:T(8,128)} %shard_map.65, f32[]{:T(128)} %constant.14.clone.1), dimensions={0}, to_apply=%region_4.5 | reduce | flops 524288 | bytes 4194308 | tf_op jit(solution)/shard_map/reduce_sum | solution.py:296
  253.0 2.4 bitcast_add_fusion
  255.5 0.8 multiply_reduce_fusion.3
  256.3 0.6 bitcast_divide_fusion
  256.9 1.2 maximum_bitcast_fusion
  (8 shorter events, 0.1 us)
Async XLA Ops:
  66.9 1.9 copy-start.2
  68.8 0.7 copy-start.3
  121.9 4.9 %copy-start.4 = (f32[3,2,16,512]{3,2,1,0:T(8,128)S(1)}, f32[3,2,16,512]{3,2,1,0:T(8,128)}, u32[]{:S(2)}) copy-start(f32[3,2,16,512]{3,2,1,0:T(8,128)} %get-tuple-element.16) | copy-start | bytes 589828
  136.7 1.9 copy-start.1
  199.9 2.0 copy-start
where the time goes:
time: 259 us; the launch traced here: 258 us
  Pallas kernels  224 us (86%)
  other arithmetic  24.9 us (10%)
  local copies, waits for them, and re-layouts  8.46 us (3%)
    pallas_call x4, Pallas kernels, exchange(): pl.pallas_call(functools.partial(exchange_kernel, n_gather, n_swap, width...  195 us
    pallas_call x3, Pallas kernels, tally(): pl.pallas_call(functools.partial(tally_kernel, per_step, iters, with_extr...  29.4 us
    reduce_sum x4, other arithmetic, body(): jnp.sum(came, axis=0)  9.64 us
    unnamed x10, local copies, waits for them, and re-layouts  6.5 us

commit v1 on v0

--- a/solution.py
+++ b/solution.py
@@ -319,6 +319,501 @@
     return (jnp.concatenate(pieces, axis=1)[None], inertia[None])
 
 
+LANES = 128
+META_ROWS = 16
+FIXED = 6
+LEVELS = 32000.0
+HALF = 32768.0
+
+
+def fused_kernel(
+    chunks, most, meta_in, emb, cents, out, inertia,
+    rows, metas, select, place_in, acc, compact, own, send, recv, inv, scale, cnt, ext,
+    ext_recv, prior, result, within,
+    load_sem, misc_sem, prior_sem, out_sem, meta_send, meta_recv, metap_send, metap_recv,
+    send_r, recv_r, send_l, recv_l, send_p, recv_p, ext_ssem, ext_rsem, swap_send, swap_recv,
+):
+    groups, shards = lax.axis_size("group"), lax.axis_size("shard")
+    chips = shards // 2
+    mine, place = lax.axis_index("group"), lax.axis_index("shard")
+    chip, core = place // 2, place % 2
+    partner = (mine, chip * 2 + 1 - core)
+    right, left = (mine, place + 2), (mine, place - 2)
+    local, block_rows, features = emb.shape
+    width = rows.shape[-1]
+    iters = place_in.shape[0]
+    owned = own.shape[2]
+    slots = local * most
+    reps = owned // LANES
+
+    def peer(step):
+        return (lax.rem(mine + step, groups), place)
+
+    def remote(src, dst, ssem, rsem, to):
+        return pltpu.make_async_remote_copy(
+            src_ref=src, dst_ref=dst, send_sem=ssem, recv_sem=rsem,
+            device_id=to, device_id_type=MESH,
+        )
+
+    def load(c):
+        return pltpu.make_async_copy(
+            emb.at[:, :, pl.ds(pl.multiple_of(c * width, width), width)],
+            rows.at[c, place], load_sem.at[c],
+        )
+
+    def load_prior(c):
+        return pltpu.make_async_copy(
+            cents.at[0, pl.ds(pl.multiple_of(place * owned, owned), owned),
+                     pl.ds(pl.multiple_of(c * width, width), width)],
+            prior.at[c], prior_sem.at[c],
+        )
+
+    meta_load = pltpu.make_async_copy(meta_in, metas.at[place], misc_sem.at[0])
+    meta_load.start()
+    for c in range(chunks):
+        load(c).start()
+
+    barrier = pltpu.get_barrier_semaphore()
+    for other in range(1, chips):
+        pl.semaphore_signal(
+            barrier, inc=1, device_id=(mine, lax.rem(chip + other, chips) * 2 + core),
+            device_id_type=MESH,
+        )
+    pl.semaphore_signal(barrier, inc=1, device_id=partner, device_id_type=MESH)
+    for step in range(1, groups):
+        pl.semaphore_signal(barrier, inc=1, device_id=peer(step), device_id_type=MESH)
+    pl.semaphore_wait(barrier, chips + groups - 1)
+
+    def meta_to(other):
+        target = lax.rem(chip + other, chips)
+        return remote(
+            metas.at[place], metas.at[place], meta_send.at[other], meta_recv.at[other],
+            (mine, target * 2 + core),
+        )
+
+    def meta_partner(q):
+        block = metas.at[q * 2 + core]
+        return remote(block, block, metap_send.at[q], metap_recv.at[q], partner)
+
+    meta_load.wait()
+    for other in range(1, chips):
+        meta_to(other).start()
+
+    def to_right(c, q):
+        block = rows.at[c, q * 2 + core]
+        return remote(block, block, send_r.at[c, chip - q], recv_r.at[c, chip - q], right)
+
+    def to_left(c, q):
+        block = rows.at[c, q * 2 + core]
+        return remote(block, block, send_l.at[c, q - chip], recv_l.at[c, q - chip], left)
+
+    def to_partner(c, q):
+        block = rows.at[c, q * 2 + core]
+        return remote(block, block, send_p.at[c, q], recv_p.at[c, q], partner)
+
+    def from_left(c, q):
+        block = rows.at[c, q * 2 + core]
+        return remote(
+            block, block, send_r.at[c, chip - 1 - q], recv_r.at[c, chip - 1 - q], right
+        )
+
+    def from_right(c, q):
+        block = rows.at[c, q * 2 + core]
+        return remote(
+            block, block, send_l.at[c, q - chip - 1], recv_l.at[c, q - chip - 1], left
+        )
+
+    def from_partner(c, q):
+        block = rows.at[c, q * 2 + 1 - core]
+        return remote(block, block, send_p.at[c, q], recv_p.at[c, q], partner)
+
+    def issue_own(c):
+        load(c).wait()
+
+        @pl.when(chip < chips - 1)
+        def _():
+            to_right(c, chip).start()
+
+        @pl.when(chip > 0)
+        def _():
+            to_left(c, chip).start()
+
+        to_partner(c, chip).start()
+
+    issue_own(0)
+    issue_own(1)
+    for c in range(chunks):
+        load_prior(c).start()
+
+    on_left, on_right = chip, chips - 1 - chip
+    both = jnp.minimum(on_left, on_right)
+
+    def source(k):
+        paired = k <= 2 * both
+        distance = jnp.where(paired, (k + 1) // 2, k - both)
+        is_left = jnp.where(paired, (k % 2) == 1, on_left > on_right)
+        return jnp.where(is_left, chip - distance, chip + distance)
+
+    ids_r = lax.broadcasted_iota(jnp.int32, (slots, block_rows), 0)
+    ids_c = lax.broadcasted_iota(jnp.int32, (owned, slots), 0)
+
+    ext[...] = jnp.zeros_like(ext)
+    acc[...] = jnp.zeros_like(acc)
+
+    def take_meta(q, core_of):
+        origin = q * 2 + core_of
+        for t in range(iters):
+            base = FIXED + 4 * t
+            wide = jnp.zeros((META_ROWS, slots), jnp.float32)
+            for b in range(local):
+                e = metas[origin, b]
+                f = e.astype(jnp.float32)
+                wanted = f[base + 2 : base + 3, :].astype(jnp.int32) == place
+                pos = jnp.where(wanted, f[base + 3 : base + 4, :].astype(jnp.int32) + b * most, -1)
+                hot = (ids_r == pos).astype(jnp.bfloat16)
+                select[origin, b, t * most : (t + 1) * most, :] = hot[b * most : (b + 1) * most, :]
+                wide = wide + lax.dot_general(
+                    e, hot, (((1,), (1,)), ((), ())), preferred_element_type=jnp.float32
+                )
+            step = wide[5:6, :].astype(jnp.int32) - mine
+            step = jnp.where(step < 0, step + groups, step)
+            label = wide[base : base + 1, :] + 256.0 * wide[base + 1 : base + 2, :]
+            cell = jnp.where(wide[0:1, :] > 0.5, step * owned + label.astype(jnp.int32), -1)
+            packed = wide.astype(jnp.bfloat16)
+            for g in range(groups):
+                hot = (ids_c == cell - g * owned).astype(jnp.bfloat16)
+                place_in[t, q, g * owned : (g + 1) * owned, core_of * slots : (core_of + 1) * slots] = hot
+                ext[g, t] += lax.dot_general(
+                    packed, hot, (((1,), (1,)), ((), ())), preferred_element_type=jnp.float32
+                )
+
+    def meta_step(k, carry):
+        q = source(k)
+
+        @pl.when(q != chip)
+        def _():
+            other = lax.rem(chip - q + chips, chips)
+            block = metas.at[q * 2 + core]
+            remote(block, block, meta_send.at[other], meta_recv.at[other], left).wait_recv()
+
+        meta_partner(q).start()
+        for core_of in range(2):
+
+            @pl.when(core_of != core)
+            def _():
+                block = metas.at[q * 2 + 1 - core]
+                remote(block, block, metap_send.at[q], metap_recv.at[q], partner).wait_recv()
+
+        for core_of in range(2):
+            take_meta(q, core_of)
+        return carry
+
+    lax.fori_loop(0, chips, meta_step, 0)
+
+    def ext_to(step):
+        return remote(
+            ext.at[step], ext_recv.at[step - 1], ext_ssem.at[step - 1], ext_rsem.at[step - 1],
+            peer(step),
+        )
+
+    for step in range(1, groups):
+        ext_to(step).start()
+
+    def tall(row):
+        return jnp.broadcast_to(row, (LANES, LANES)).T
+
+    for step in range(1, groups):
+        for t in range(iters):
+            for i in range(reps):
+                bound = ext[step, t, 4:5, i * LANES : (i + 1) * LANES]
+                inv[step - 1, t, i * LANES : (i + 1) * LANES, :] = tall(
+                    LEVELS / jnp.maximum(bound, 1e-30)
+                )
+
+    def swap(c, step):
+        return remote(
+            send.at[c, step - 1], recv.at[c, step - 1], swap_send.at[c, step - 1],
+            swap_recv.at[c, step - 1], peer(step),
+        )
+
+    tile = owned
+
+    def tally(c, q, first):
+        for core_of in range(2):
+            origin = q * 2 + core_of
+            for b in range(local):
+                got = jnp.dot(
+                    select[origin, b], rows[c, origin, b], preferred_element_type=jnp.float32
+                ).astype(jnp.bfloat16)
+                for t in range(iters):
+                    compact[t, core_of * slots + b * most : core_of * slots + (b + 1) * most, :] = got[
+                        t * most : (t + 1) * most, :
+                    ]
+
+        def body(i, carry):
+            for t in range(iters):
+                part = pl.ds(pl.multiple_of(i * tile, tile), tile)
+                acc[t, part, :] += jnp.dot(
+                    place_in[t, q, part, :], compact[t], preferred_element_type=jnp.float32
+                )
+            return carry
+
+        lax.fori_loop(0, groups, body, 0)
+
+    def settle(c):
+        for t in range(iters):
+            own[c, t] = acc[t, :owned, :]
+        for step in range(1, groups):
+            part = slice(step * owned, (step + 1) * owned)
+            high = (acc[0, part, :] * inv[step - 1, 0] + (HALF + 0.5)).astype(jnp.int32)
+            low = (acc[1, part, :] * inv[step - 1, 1] + (HALF + 0.5)).astype(jnp.int32)
+            send[c, step - 1] = (high << 16) | low
+            swap(c, step).start()
+        acc[...] = jnp.zeros_like(acc)
+
+    def scales():
+        for step in range(1, groups):
+            ext_to(step).wait_recv()
+        for t in range(iters):
+            for i in range(reps):
+                part = slice(i * LANES, (i + 1) * LANES)
+                count = ext[0, t, 0:1, part]
+                for step in range(1, groups):
+                    count = count + ext_recv[step - 1, t, 0:1, part]
+                    scale[step - 1, t, part, :] = tall(ext_recv[step - 1, t, 4:5, part] / LEVELS)
+                cnt[t, part, :] = tall(count)
+        within[...] = jnp.zeros_like(within)
+
+    def finish(c):
+        load_prior(c).wait()
+        for step in range(1, groups):
+            swap(c, step).wait_recv()
+        for i in range(reps):
+            part = slice(i * LANES, (i + 1) * LANES)
+            sums = [own[c, t, part, :] for t in range(iters)]
+            for step in range(1, groups):
+                word = recv[c, step - 1, part, :]
+                high = lax.shift_right_logical(word, 16)
+                low = word & 0xFFFF
+                for t, code in enumerate((high, low)):
+                    sums[t] = sums[t] + (code.astype(jnp.float32) - HALF) * scale[step - 1, t, part, :]
+            previous = prior[c, part, :]
+            for t in range(iters):
+                count = cnt[t, part, :]
+                if t == iters - 1:
+                    within[part, :] += previous * (count * previous - 2.0 * sums[t])
+                previous = (sums[t] + PRIOR * previous) / (count + PRIOR)
+            result[c, part, :] = previous
+
+    def store(c):
+        return pltpu.make_async_copy(
+            result.at[c], out.at[:, pl.ds(pl.multiple_of(c * width, width), width)], out_sem.at[c]
+        )
+
+    def main_step(j, carry):
+        c, k = j // chips, j % chips
+        q = source(k)
+
+        @pl.when((k == 0) & (c + 2 < chunks))
+        def _():
+            issue_own(c + 2)
+
+        @pl.when(q < chip)
+        def _():
+            from_left(c, q).wait_recv()
+
+            @pl.when(chip < chips - 1)
+            def _():
+                to_right(c, q).start()
+
+            to_partner(c, q).start()
+
+        @pl.when(q > chip)
+        def _():
+            from_right(c, q).wait_recv()
+
+            @pl.when(chip > 0)
+            def _():
+                to_left(c, q).start()
+
+            to_partner(c, q).start()
+
+        from_partner(c, q).wait_recv()
+        tally(c, q, k == 0)
+
+        @pl.when(k == chips - 1)
+        def _():
+            settle(c)
+
+            @pl.when(c == 0)
+            def _():
+                scales()
+
+            @pl.when(c > 0)
+            def _():
+                finish(c - 1)
+                store(c - 1).start()
+
+        return carry
+
+    lax.fori_loop(0, chunks * chips, main_step, 0)
+    finish(chunks - 1)
+    store(chunks - 1).start()
+
+    for i in range(reps):
+        part = slice(i * LANES, (i + 1) * LANES)
+        spread = jnp.sum(within[part, :].T, axis=0, keepdims=True)
+        last = iters - 1
+        count = ext[0, last, 0:1, part]
+        square = ext[0, last, 1:2, part] + ext[0, last, 2:3, part] + ext[0, last, 3:4, part]
+        for step in range(1, groups):
+            far = ext_recv[step - 1, last, :, part]
+            count = count + far[0:1]
+            square = square + far[1:2] + far[2:3] + far[3:4]
+        inertia[:, part] = (spread + square) / ((count + PRIOR) * features)
+
+    for other in range(1, chips):
+        meta_to(other).wait_send()
+    for q in range(chips):
+        meta_partner(q).wait_send()
+    for step in range(1, groups):
+        ext_to(step).wait_send()
+
+    def drain(j, carry):
+        c, q = j // chips, j % chips
+
+        @pl.when((q <= chip) & (chip < chips - 1))
+        def _():
+            to_right(c, q).wait_send()
+
+        @pl.when((q >= chip) & (chip > 0))
+        def _():
+            to_left(c, q).wait_send()
+
+        to_partner(c, q).wait_send()
+        return carry
+
+    lax.fori_loop(0, chunks * chips, drain, 0)
+    for c in range(chunks):
+        for step in range(1, groups):
+            swap(c, step).wait_send()
+        store(c).wait()
+
+
+def fused_buffers(local, block_rows, features, iters, owned, groups, shards):
+    chips = shards // 2
+    most = 2 * block_rows // shards
+    width, chunks = LANES, features // LANES
+    slots = local * most
+    vmem = pltpu.VMEM
+    f32, b16, i32 = jnp.float32, jnp.bfloat16, jnp.int32
+    buffers = [
+        ((chunks, shards, local, block_rows, width), b16),
+        ((shards, local, META_ROWS, block_rows), b16),
+        ((shards, local, iters * most, block_rows), b16),
+        ((iters, chips, groups * owned, 2 * slots), b16),
+        ((iters, groups * owned, width), f32),
+        ((iters, 2 * slots, width), b16),
+        ((chunks, iters, owned, width), f32),
+        ((chunks, groups - 1, owned, width), i32),
+        ((chunks, groups - 1, owned, width), i32),
+        ((groups - 1, iters, owned, width), f32),
+        ((groups - 1, iters, owned, width), f32),
+        ((iters, owned, width), f32),
+        ((groups, iters, META_ROWS, owned), f32),
+        ((groups - 1, iters, META_ROWS, owned), f32),
+        ((chunks, owned, width), f32),
+        ((chunks, owned, width), f32),
+        ((owned, width), f32),
+    ]
+    dma = pltpu.SemaphoreType.DMA
+    sems = [dma((chunks,)), dma((1,)), dma((chunks,)), dma((chunks,))]
+    sems += [dma((chips,))] * 4
+    sems += [dma((chunks, chips))] * 6
+    sems += [dma((groups - 1,))] * 2
+    sems += [dma((chunks, groups - 1))] * 2
+    return [vmem(s, d) for s, d in buffers], sems, buffers, most, chunks
+
+
+def fits(local, block_rows, features, iters, owned, groups, shards):
+    if features % LANES or features < 2 * LANES or owned % LANES or shards % 2:
+        return False
+    if iters != 2 or 4 * iters + FIXED > META_ROWS or (2 * block_rows) % shards:
+        return False
+    most = 2 * block_rows // shards
+    if (local * most) % LANES or most % 16 or block_rows % LANES:
+        return False
+    total = 0
+    for shape, dtype in fused_buffers(local, block_rows, features, iters, owned, groups, shards)[2]:
+        size = jnp.dtype(dtype).itemsize
+        for extent in shape:
+            size *= extent
+        total += size
+    return total < 58 * 2**20
+
+
+def fused_body(embeddings, assignments, block_group, centroids):
+    groups, shards = lax.axis_size("group"), lax.axis_size("shard")
+    local, block_rows, features = embeddings.shape
+    iters = assignments.shape[1]
+    owned = centroids.shape[1] // shards
+    buffers, sems, unused, most, chunks = fused_buffers(
+        local, block_rows, features, iters, owned, groups, shards
+    )
+
+    wide = embeddings.astype(jnp.float32)
+    square = jnp.sum(wide * wide, axis=2)
+    peak = jnp.max(jnp.abs(wide), axis=2)
+    high = lax.reduce_precision(square, 8, 7)
+    middle = lax.reduce_precision(square - high, 8, 7)
+    low = square - high - middle
+    ranges = assignments // owned
+    inside = (assignments % owned)
+    hot = (ranges[:, :, None, :] == jnp.arange(shards)[:, None]).astype(jnp.bfloat16)
+    before = (jnp.arange(block_rows)[:, None] < jnp.arange(block_rows)[None, :]).astype(jnp.bfloat16)
+    earlier = jnp.dot(hot.reshape(-1, block_rows), before, preferred_element_type=jnp.float32)
+    rank = jnp.sum(earlier.reshape(hot.shape) * hot.astype(jnp.float32), axis=2)
+    one = jnp.ones_like(square)
+    owner = jnp.broadcast_to(block_group[:, None].astype(jnp.float32), square.shape)
+    lines = [one, high, middle, low, peak, owner]
+    for t in range(iters):
+        lines += [
+            (inside[:, t] % 256).astype(jnp.float32),
+            (inside[:, t] // 256).astype(jnp.float32),
+            ranges[:, t].astype(jnp.float32),
+            rank[:, t],
+        ]
+    lines += [jnp.zeros_like(square)] * (META_ROWS - len(lines))
+    meta = jnp.stack(lines, axis=1).astype(jnp.bfloat16)
+
+    out, inertia = pl.pallas_call(
+        functools.partial(fused_kernel, chunks, most),
+        out_shape=[
+            jax.ShapeDtypeStruct((owned, features), jnp.float32),
+            jax.ShapeDtypeStruct((1, owned), jnp.float32),
+        ],
+        in_specs=[pl.BlockSpec(memory_space=pl.ANY)] * 3,
+        out_specs=[
+            pl.BlockSpec(memory_space=pl.ANY),
+            pl.BlockSpec(memory_space=pltpu.VMEM),
+        ],
+        scratch_shapes=buffers + sems,
+        compiler_params=pltpu.CompilerParams(
+            collective_id=0, has_side_effects=True, vmem_limit_bytes=63 * 2**20
+        ),
+    )(meta, embeddings, centroids)
+    return out[None], inertia
+
+
+def choose(embeddings, assignments, block_group, centroids):
+    groups, shards = lax.axis_size("group"), lax.axis_size("shard")
+    local, block_rows, features = embeddings.shape
+    owned = centroids.shape[1] // shards
+    if fits(local, block_rows, features, assignments.shape[1], owned, groups, shards):
+        return fused_body(embeddings, assignments, block_group, centroids)
+    return body(embeddings, assignments, block_group, centroids)
+
+
 def solution(mesh):
     in_specs = (
         P(("group", "shard"), None, None),
@@ -327,4 +822,4 @@
         P("group", None, None),
     )
     out_specs = (P("group", "shard", None), P("group", "shard"))
-    return jax.shard_map(body, mesh=mesh, in_specs=in_specs, out_specs=out_specs, check_vma=False)
+    return jax.shard_map(choose, mesh=mesh, in_specs=in_specs, out_specs=out_specs, check_vma=False)

time: 259 us -> 157 us (0.61)
  Pallas kernels: 224 us -> 148 us
  other arithmetic: 24.9 us -> 3.52 us
  local copies, waits for them, and re-layouts: 8.46 us -> 4.66 us
    pallas_call x7 -> x1, Pallas kernels: 224 us -> 148 us  [fused_body(): pl.pallas_call(functools.partial(fused_kernel, chunks, most), out_shape=[...]
    reduce_sum x6 -> x0, other arithmetic: 12.2 us -> none  [the longest x4 9.64 us: body(): jnp.sum(came, axis=0)]
    add x5 -> x0, other arithmetic: 4.98 us -> none  [the longest x3 4.98 us: body(): lax.dynamic_index_in_dim(kept, mine, 0, keepdims=False)]
    unnamed x10 -> x4, local copies, waits for them, and re-layouts: 6.5 us -> 3.23 us
    convert_element_type x3 -> x0, other arithmetic: 2.93 us -> none  [the longest x1 1.57 us: body(): owners = metas[:, iters, 0].astype(jnp.int32)]
where the time goes in v1:
time: 157 us
  Pallas kernels  148 us (94%)
  local copies, waits for them, and re-layouts  4.66 us (3%)
  other arithmetic  3.52 us (2%)
    pallas_call x1, Pallas kernels, fused_body(): pl.pallas_call(functools.partial(fused_kernel, chunks, most), out_shape=[...  148 us
    unnamed x4, local copies, waits for them, and re-layouts  3.23 us

profile of v1, /device:TPU:0, one launch (start us, length us, event | category | flops | bytes accessed | tf_op | source)
XLA Modules:
  0.0 156.8 jit_solution(14033943176438705645)
XLA Ops:
  0.6 0.7 convert_convert_fusion.2
  1.3 0.1 stack_broadcast_in_dim.9
  1.4 2.0 %fusion.1 = (bf16[4,256]{1,0:T(4,128)(2,1)S(1)}, f32[4,256]{1,0:T(4,128)S(1)}) fusion(bf16[4,256,768]{2,1,0:T(8,128)(2,1)} %emb.1), kind=kLoop, calls=%fused_computation.3 | loop fusion | flops 3930112 | bytes 1579008 | tf_op jit(solution)/shard_map/reduce_max | solution.py:766
  3.4 0.7 and_select_fusion.2
  4.2 0.2 fusion.2
  4.4 0.1 fusion.12
  4.5 1.3 stack.10.meta_in
  5.8 147.8 %shard_map.59 = (f32[512,768]{1,0:T(8,128)}, f32[1,512]{1,0:T(1,128)}) custom-call(bf16[4,16,256]{2,1,0:T(8,128)(2,1)} %stack.10.meta_in, bf16[4,256,768]{2,1,0:T(8,128)(2,1)} %emb.1, f32[1,4096,768]{2,1,0:T(8,128)} %cents.1), custom_call_target="tpu_custom_call" | custom-call | tf_op jit(solution)/shard_map/pallas_call | solution.py:789
  153.6 0.0 copy-start
  153.6 2.7 %copy.11 = f32[1,512,768]{2,1,0:T(8,128)} copy(f32[1,512,768]{2,1,0:T(8,128)} %bitcast.9) | data formatting | bytes 3145728
  156.3 0.0 copy-done
  156.3 0.6 copy.12
  (7 shorter events, 0.1 us)
Async XLA Ops:
  153.6 2.7 %copy-start = (f32[1,512]{1,0:T(1,128)S(1)}, f32[1,512]{1,0:T(1,128)}, u32[]{:S(2)}) copy-start(f32[1,512]{1,0:T(1,128)} %get-tuple-element.30) | copy-start | bytes 6148

commit v2 on v1

--- a/solution.py
+++ b/solution.py
@@ -327,10 +327,10 @@
 
 
 def fused_kernel(
-    chunks, most, meta_in, emb, cents, out, inertia,
+    chunks, most, owner_in, label_in, emb, cents, out, inertia,
     rows, metas, select, place_in, acc, compact, own, send, recv, inv, scale, cnt, ext,
-    ext_recv, prior, result, within,
-    load_sem, misc_sem, prior_sem, out_sem, meta_send, meta_recv, metap_send, metap_recv,
+    ext_recv, prior, within, lines,
+    load_sem, prior_sem, meta_send, meta_recv, metap_send, metap_recv,
     send_r, recv_r, send_l, recv_l, send_p, recv_p, ext_ssem, ext_rsem, swap_send, swap_recv,
 ):
     groups, shards = lax.axis_size("group"), lax.axis_size("shard")
@@ -368,8 +368,6 @@
             prior.at[c], prior_sem.at[c],
         )
 
-    meta_load = pltpu.make_async_copy(meta_in, metas.at[place], misc_sem.at[0])
-    meta_load.start()
     for c in range(chunks):
         load(c).start()
 
@@ -395,10 +393,6 @@
         block = metas.at[q * 2 + core]
         return remote(block, block, metap_send.at[q], metap_recv.at[q], partner)
 
-    meta_load.wait()
-    for other in range(1, chips):
-        meta_to(other).start()
-
     def to_right(c, q):
         block = rows.at[c, q * 2 + core]
         return remote(block, block, send_r.at[c, chip - q], recv_r.at[c, chip - q], right)
@@ -428,8 +422,6 @@
         return remote(block, block, send_p.at[c, q], recv_p.at[c, q], partner)
 
     def issue_own(c):
-        load(c).wait()
-
         @pl.when(chip < chips - 1)
         def _():
             to_right(c, chip).start()
@@ -440,10 +432,59 @@
 
         to_partner(c, chip).start()
 
+    load(0).wait()
     issue_own(0)
-    issue_own(1)
     for c in range(chunks):
         load_prior(c).start()
+    for c in range(1, chunks):
+        load(c).wait()
+
+    ids_s = lax.broadcasted_iota(jnp.int32, (shards, block_rows), 0).astype(jnp.float32)
+    before = (
+        lax.broadcasted_iota(jnp.int32, (block_rows, block_rows), 0)
+        < lax.broadcasted_iota(jnp.int32, (block_rows, block_rows), 1)
+    ).astype(jnp.bfloat16)
+    labels = [[label_in[b, t : t + 1, :].astype(jnp.float32) for t in range(iters)] for b in range(local)]
+    ranges = [[jnp.floor((x + 0.5) * (1.0 / owned)) for x in xs] for xs in labels]
+    hots = [[(ids_s == x).astype(jnp.float32) for x in xs] for xs in ranges]
+    flat = [x for xs in hots for x in xs]
+    earlier = jnp.dot(
+        jnp.concatenate(flat, axis=0).astype(jnp.bfloat16), before,
+        preferred_element_type=jnp.float32,
+    )
+    lines[...] = jnp.zeros_like(lines)
+    for b in range(local):
+        total = jnp.zeros((block_rows, width), jnp.float32)
+        top = jnp.zeros((block_rows, width), jnp.float32)
+        for c in range(chunks):
+            x = rows[c, place, b].astype(jnp.float32)
+            total = total + x * x
+            top = jnp.maximum(top, jnp.abs(x))
+        square = jnp.sum(total.T, axis=0, keepdims=True)
+        high = square.astype(jnp.bfloat16).astype(jnp.float32)
+        middle = (square - high).astype(jnp.bfloat16).astype(jnp.float32)
+        lines[0:1, :] = jnp.ones_like(square)
+        lines[1:2, :] = high
+        lines[2:3, :] = middle
+        lines[3:4, :] = square - high - middle
+        lines[4:5, :] = jnp.max(top.T, axis=0, keepdims=True)
+        lines[5:6, :] = jnp.full((1, block_rows), owner_in[b], jnp.int32).astype(jnp.float32)
+        for t in range(iters):
+            base = FIXED + 4 * t
+            inside = labels[b][t] - ranges[b][t] * owned
+            coarse = jnp.floor((inside + 0.5) * (1.0 / 256))
+            at = (b * iters + t) * shards
+            lines[base : base + 1, :] = inside - 256.0 * coarse
+            lines[base + 1 : base + 2, :] = coarse
+            lines[base + 2 : base + 3, :] = ranges[b][t]
+            lines[base + 3 : base + 4, :] = jnp.sum(
+                hots[b][t] * earlier[at : at + shards, :], axis=0, keepdims=True
+            )
+        metas[place, b] = lines[...].astype(jnp.bfloat16)
+
+    for other in range(1, chips):
+        meta_to(other).start()
+    issue_own(1)
 
     on_left, on_right = chip, chips - 1 - chip
     both = jnp.minimum(on_left, on_right)
@@ -453,6 +494,34 @@
         distance = jnp.where(paired, (k + 1) // 2, k - both)
         is_left = jnp.where(paired, (k % 2) == 1, on_left > on_right)
         return jnp.where(is_left, chip - distance, chip + distance)
+
+    def pull(j):
+        c, k = j // chips, j % chips
+        q = source(k)
+
+        @pl.when((k == 0) & (c + 2 < chunks))
+        def _():
+            issue_own(c + 2)
+
+        @pl.when(q < chip)
+        def _():
+            from_left(c, q).wait_recv()
+
+            @pl.when(chip < chips - 1)
+            def _():
+                to_right(c, q).start()
+
+            to_partner(c, q).start()
+
+        @pl.when(q > chip)
+        def _():
+            from_right(c, q).wait_recv()
+
+            @pl.when(chip > 0)
+            def _():
+                to_left(c, q).start()
+
+            to_partner(c, q).start()
 
     ids_r = lax.broadcasted_iota(jnp.int32, (slots, block_rows), 0)
     ids_c = lax.broadcasted_iota(jnp.int32, (owned, slots), 0)
@@ -506,6 +575,7 @@
 
         for core_of in range(2):
             take_meta(q, core_of)
+        pull(k)
         return carry
 
     lax.fori_loop(0, chips, meta_step, 0)
@@ -603,40 +673,16 @@
                 if t == iters - 1:
                     within[part, :] += previous * (count * previous - 2.0 * sums[t])
                 previous = (sums[t] + PRIOR * previous) / (count + PRIOR)
-            result[c, part, :] = previous
-
-    def store(c):
-        return pltpu.make_async_copy(
-            result.at[c], out.at[:, pl.ds(pl.multiple_of(c * width, width), width)], out_sem.at[c]
-        )
+            out[part, pl.ds(pl.multiple_of(c * width, width), width)] = previous
 
     def main_step(j, carry):
         c, k = j // chips, j % chips
         q = source(k)
-
-        @pl.when((k == 0) & (c + 2 < chunks))
-        def _():
-            issue_own(c + 2)
-
-        @pl.when(q < chip)
-        def _():
-            from_left(c, q).wait_recv()
-
-            @pl.when(chip < chips - 1)
-            def _():
-                to_right(c, q).start()
-
-            to_partner(c, q).start()
-
-        @pl.when(q > chip)
-        def _():
-            from_right(c, q).wait_recv()
-
-            @pl.when(chip > 0)
-            def _():
-                to_left(c, q).start()
-
-            to_partner(c, q).start()
+        ahead = j + jnp.where(both > 0, chips, 0)
+
+        @pl.when((ahead >= chips) & (ahead < chunks * chips))
+        def _():
+            pull(ahead)
 
         from_partner(c, q).wait_recv()
         tally(c, q, k == 0)
@@ -652,13 +698,11 @@
             @pl.when(c > 0)
             def _():
                 finish(c - 1)
-                store(c - 1).start()
 
         return carry
 
     lax.fori_loop(0, chunks * chips, main_step, 0)
     finish(chunks - 1)
-    store(chunks - 1).start()
 
     for i in range(reps):
         part = slice(i * LANES, (i + 1) * LANES)
@@ -697,7 +741,6 @@
     for c in range(chunks):
         for step in range(1, groups):
             swap(c, step).wait_send()
-        store(c).wait()
 
 
 def fused_buffers(local, block_rows, features, iters, owned, groups, shards):
@@ -723,11 +766,11 @@
         ((groups, iters, META_ROWS, owned), f32),
         ((groups - 1, iters, META_ROWS, owned), f32),
         ((chunks, owned, width), f32),
-        ((chunks, owned, width), f32),
         ((owned, width), f32),
+        ((META_ROWS, block_rows), f32),
     ]
     dma = pltpu.SemaphoreType.DMA
-    sems = [dma((chunks,)), dma((1,)), dma((chunks,)), dma((chunks,))]
+    sems = [dma((chunks,)), dma((chunks,))]
     sems += [dma((chips,))] * 4
     sems += [dma((chunks, chips))] * 6
     sems += [dma((groups - 1,))] * 2
@@ -761,47 +804,24 @@
         local, block_rows, features, iters, owned, groups, shards
     )
 
-    wide = embeddings.astype(jnp.float32)
-    square = jnp.sum(wide * wide, axis=2)
-    peak = jnp.max(jnp.abs(wide), axis=2)
-    high = lax.reduce_precision(square, 8, 7)
-    middle = lax.reduce_precision(square - high, 8, 7)
-    low = square - high - middle
-    ranges = assignments // owned
-    inside = (assignments % owned)
-    hot = (ranges[:, :, None, :] == jnp.arange(shards)[:, None]).astype(jnp.bfloat16)
-    before = (jnp.arange(block_rows)[:, None] < jnp.arange(block_rows)[None, :]).astype(jnp.bfloat16)
-    earlier = jnp.dot(hot.reshape(-1, block_rows), before, preferred_element_type=jnp.float32)
-    rank = jnp.sum(earlier.reshape(hot.shape) * hot.astype(jnp.float32), axis=2)
-    one = jnp.ones_like(square)
-    owner = jnp.broadcast_to(block_group[:, None].astype(jnp.float32), square.shape)
-    lines = [one, high, middle, low, peak, owner]
-    for t in range(iters):
-        lines += [
-            (inside[:, t] % 256).astype(jnp.float32),
-            (inside[:, t] // 256).astype(jnp.float32),
-            ranges[:, t].astype(jnp.float32),
-            rank[:, t],
-        ]
-    lines += [jnp.zeros_like(square)] * (META_ROWS - len(lines))
-    meta = jnp.stack(lines, axis=1).astype(jnp.bfloat16)
-
     out, inertia = pl.pallas_call(
         functools.partial(fused_kernel, chunks, most),
         out_shape=[
-            jax.ShapeDtypeStruct((owned, features), jnp.float32),
-            jax.ShapeDtypeStruct((1, owned), jnp.float32),
+            pltpu.VMEM((owned, features), jnp.float32),
+            pltpu.VMEM((1, owned), jnp.float32),
         ],
-        in_specs=[pl.BlockSpec(memory_space=pl.ANY)] * 3,
-        out_specs=[
+        in_specs=[
+            pl.BlockSpec(memory_space=pltpu.SMEM),
+            pl.BlockSpec(memory_space=pltpu.VMEM),
             pl.BlockSpec(memory_space=pl.ANY),
-            pl.BlockSpec(memory_space=pltpu.VMEM),
+            pl.BlockSpec(memory_space=pl.ANY),
         ],
+        out_specs=[pl.BlockSpec(memory_space=pltpu.VMEM)] * 2,
         scratch_shapes=buffers + sems,
         compiler_params=pltpu.CompilerParams(
-            collective_id=0, has_side_effects=True, vmem_limit_bytes=63 * 2**20
+            collective_id=0, has_side_effects=True, vmem_limit_bytes=56 * 2**20
         ),
-    )(meta, embeddings, centroids)
+    )(block_group, assignments, embeddings, centroids)
     return out[None], inertia
 
 

time: 157 us -> 139 us (0.89)
  Pallas kernels: 148 us -> 137 us
  other arithmetic: 3.52 us -> 0 us
  local copies, waits for them, and re-layouts: 4.66 us -> 1.72 us
    pallas_call x1, Pallas kernels: 148 us -> 137 us  [fused_body(): pl.pallas_call(functools.partial(fused_kernel, chunks, most), out_shape=[...]
    reduce_max x1 -> x0, other arithmetic: 2.04 us -> none  [fused_body(): peak = jnp.max(jnp.abs(wide), axis=2)]
    unnamed x4 -> x2, local copies, waits for them, and re-layouts: 3.23 us -> 1.72 us
where the time goes in v2:
time: 139 us
  Pallas kernels  137 us (99%)
  local copies, waits for them, and re-layouts  1.72 us (1%)
    pallas_call x1, Pallas kernels, fused_body(): pl.pallas_call(functools.partial(fused_kernel, chunks, most), out_shape=[...  137 us

profile of v2, /device:TPU:0, one launch (start us, length us, event | category | flops | bytes accessed | tf_op | source)
XLA Modules:
  0.0 139.0 jit_solution(4853419103160291447)
XLA Ops:
  0.6 136.7 %shard_map.59 = (f32[512,768]{1,0:T(8,128)S(1)}, f32[1,512]{1,0:T(1,128)S(1)}) custom-call(s32[4]{0:T(128)} %owner_in.1, s32[4,2,256]{2,1,0:T(2,128)} %label_in.1, bf16[4,256,768]{2,1,0:T(8,128)(2,1)} %emb.1, f32[1,4096,768]{2,1,0:T(8,128)} %cents.1), custom_call_target="tpu_custom_call" | custom-call | tf_op jit(solution)/shard_map/pallas_call | solution.py:807
  137.3 1.1 copy.8
  138.4 0.6 copy.9

commit v3 on v2

--- a/solution.py
+++ b/solution.py
@@ -322,16 +322,21 @@
 LANES = 128
 META_ROWS = 16
 FIXED = 6
+CAP = 2
 LEVELS = 32000.0
 HALF = 32768.0
 
 
 def fused_kernel(
-    chunks, most, owner_in, label_in, emb, cents, out, inertia,
+    chunks, late, most, owner_in, label_in, emb, cents, out, inertia,
     rows, metas, select, place_in, acc, compact, own, send, recv, inv, scale, cnt, ext,
-    ext_recv, prior, within, lines,
+    ext_recv, prior, within, lines, share,
+    late_own, late_send, late_rows, late_meta_send, late_metas, late_select, late_cells, late_compact,
+    late_acc, late_out, late_in, late_scale_out, late_scale_in,
     load_sem, prior_sem, meta_send, meta_recv, metap_send, metap_recv,
     send_r, recv_r, send_l, recv_l, send_p, recv_p, ext_ssem, ext_rsem, swap_send, swap_recv,
+    late_load_sem, lswap_s, lswap_r, lpart_s, lpart_r, lin_s, lin_r, lshare_s, lshare_r,
+    code_s, code_r, scale_s, scale_r,
 ):
     groups, shards = lax.axis_size("group"), lax.axis_size("shard")
     chips = shards // 2
@@ -339,11 +344,14 @@
     chip, core = place // 2, place % 2
     partner = (mine, chip * 2 + 1 - core)
     right, left = (mine, place + 2), (mine, place - 2)
+    is_end = (chip == 0) | (chip == chips - 1)
+    mate = chip + 1 - 2 * lax.rem(chip, 2)
+    targets = [place, (chips - 1 - chip) * 2 + core, (chips - 1 - mate) * 2 + core, mate * 2 + core]
     local, block_rows, features = emb.shape
     width = rows.shape[-1]
     iters = place_in.shape[0]
     owned = own.shape[2]
-    slots = local * most
+    slots = CAP * most
     reps = owned // LANES
 
     def peer(step):
@@ -359,6 +367,12 @@
         return pltpu.make_async_copy(
             emb.at[:, :, pl.ds(pl.multiple_of(c * width, width), width)],
             rows.at[c, place], load_sem.at[c],
+        )
+
+    def load_late(x):
+        at = (chunks + x) * width
+        return pltpu.make_async_copy(
+            emb.at[:, :, pl.ds(at, width)], late_own.at[x], late_load_sem.at[x]
         )
 
     def load_prior(c):
@@ -370,6 +384,8 @@
 
     for c in range(chunks):
         load(c).start()
+    for x in range(late):
+        load_late(x).start()
 
     barrier = pltpu.get_barrier_semaphore()
     for other in range(1, chips):
@@ -433,11 +449,14 @@
         to_partner(c, chip).start()
 
     load(0).wait()
+    load(1).wait()
     issue_own(0)
-    for c in range(chunks):
+    for c in range(chunks + late):
         load_prior(c).start()
-    for c in range(1, chunks):
+    for c in range(2, chunks):
         load(c).wait()
+    for x in range(late):
+        load_late(x).wait()
 
     ids_s = lax.broadcasted_iota(jnp.int32, (shards, block_rows), 0).astype(jnp.float32)
     before = (
@@ -456,8 +475,9 @@
     for b in range(local):
         total = jnp.zeros((block_rows, width), jnp.float32)
         top = jnp.zeros((block_rows, width), jnp.float32)
-        for c in range(chunks):
-            x = rows[c, place, b].astype(jnp.float32)
+        for c in range(chunks + late):
+            x = rows[c, place, b] if c < chunks else late_own[c - chunks, b]
+            x = x.astype(jnp.float32)
             total = total + x * x
             top = jnp.maximum(top, jnp.abs(x))
         square = jnp.sum(total.T, axis=0, keepdims=True)
@@ -468,7 +488,10 @@
         lines[2:3, :] = middle
         lines[3:4, :] = square - high - middle
         lines[4:5, :] = jnp.max(top.T, axis=0, keepdims=True)
-        lines[5:6, :] = jnp.full((1, block_rows), owner_in[b], jnp.int32).astype(jnp.float32)
+        turn = owner_in[b] * CAP
+        for other in range(b):
+            turn = turn + jnp.where(owner_in[other] == owner_in[b], 1, 0)
+        lines[5:6, :] = jnp.full((1, block_rows), turn, jnp.int32).astype(jnp.float32)
         for t in range(iters):
             base = FIXED + 4 * t
             inside = labels[b][t] - ranges[b][t] * owned
@@ -486,6 +509,78 @@
         meta_to(other).start()
     issue_own(1)
 
+    def late_swap(x, step):
+        sent = late_meta_send if x == late else late_send.at[x]
+        kept = late_metas if x == late else late_rows.at[x]
+        return remote(
+            sent.at[step - 1], kept.at[core, step], lswap_s.at[x, step - 1],
+            lswap_r.at[x, step - 1], peer(step),
+        )
+
+    def late_block(x, at):
+        return late_metas.at[at] if x == late else late_rows.at[x, at]
+
+    def late_partner(x):
+        block = late_block(x, core)
+        return remote(block, block, lpart_s.at[x], lpart_r.at[x], partner)
+
+    def late_inward(x):
+        return remote(
+            late_block(x, core), late_block(x, 2 + core), lin_s.at[x], lin_r.at[x],
+            (mine, mate * 2 + core),
+        )
+
+    def late_share(x):
+        block = late_block(x, 2 + core)
+        return remote(block, block, lshare_s.at[x], lshare_r.at[x], partner)
+
+    def late_start():
+        for x in (late,) + tuple(range(late)):
+            for step in range(1, groups):
+                late_swap(x, step).wait_recv()
+            late_partner(x).start()
+
+            @pl.when(is_end)
+            def _():
+                late_inward(x).start()
+
+    chosen = []
+    for b in range(local):
+        turn = metas[place, b].astype(jnp.float32)[5:6, :LANES].astype(jnp.int32) - mine * CAP
+        chosen.append(jnp.where(turn < 0, turn + groups * CAP, turn))
+    for step in range(groups):
+        for i in range(CAP):
+            weights = [
+                jnp.broadcast_to(
+                    (turn == step * CAP + i).astype(jnp.float32), (META_ROWS, LANES)
+                ).astype(jnp.bfloat16)
+                for turn in chosen
+            ]
+
+            def pick(blocks):
+                tiles = [x.reshape(x.shape[0] // META_ROWS, META_ROWS, LANES) for x in blocks]
+                put = tiles[0] * weights[0][None]
+                for b in range(1, local):
+                    put = put + tiles[b] * weights[b][None]
+                return put.reshape(blocks[0].shape)
+
+            for lane in range(0, block_rows, LANES):
+                part = slice(lane, lane + LANES)
+                put = pick([metas[place, b, :, part] for b in range(local)])
+                if step == 0:
+                    late_metas[core, 0, i, :, part] = put
+                else:
+                    late_meta_send[step - 1, i, :, part] = put
+            for x in range(late):
+                put = pick([late_own[x, b] for b in range(local)])
+                if step == 0:
+                    late_rows[x, core, 0, i] = put
+                else:
+                    late_send[x, step - 1, i] = put
+    for x in (late,) + tuple(range(late)):
+        for step in range(1, groups):
+            late_swap(x, step).start()
+
     on_left, on_right = chip, chips - 1 - chip
     both = jnp.minimum(on_left, on_right)
 
@@ -523,37 +618,51 @@
 
             to_partner(c, q).start()
 
-    ids_r = lax.broadcasted_iota(jnp.int32, (slots, block_rows), 0)
+    ids_m = lax.rem(lax.broadcasted_iota(jnp.int32, (slots, block_rows), 0), most)
     ids_c = lax.broadcasted_iota(jnp.int32, (owned, slots), 0)
+    turns = lax.broadcasted_iota(jnp.int32, (1, slots), 1) // most
 
     ext[...] = jnp.zeros_like(ext)
     acc[...] = jnp.zeros_like(acc)
+    late_acc[...] = jnp.zeros_like(late_acc)
+    late_scale_out[...] = jnp.zeros_like(late_scale_out)
 
     def take_meta(q, core_of):
         origin = q * 2 + core_of
+        rel = []
+        for b in range(local):
+            place_of = metas[origin, b].astype(jnp.float32)[5:6, :slots].astype(jnp.int32) - mine * CAP
+            rel.append(jnp.where(place_of < 0, place_of + groups * CAP, place_of))
+            for i in range(groups * CAP):
+                one = (rel[b] == i).astype(jnp.float32)[:, :LANES]
+                share[origin, b, i] = jnp.broadcast_to(one, (16, LANES)).astype(jnp.bfloat16)
         for t in range(iters):
             base = FIXED + 4 * t
-            wide = jnp.zeros((META_ROWS, slots), jnp.float32)
+            found = []
             for b in range(local):
                 e = metas[origin, b]
                 f = e.astype(jnp.float32)
                 wanted = f[base + 2 : base + 3, :].astype(jnp.int32) == place
-                pos = jnp.where(wanted, f[base + 3 : base + 4, :].astype(jnp.int32) + b * most, -1)
-                hot = (ids_r == pos).astype(jnp.bfloat16)
-                select[origin, b, t * most : (t + 1) * most, :] = hot[b * most : (b + 1) * most, :]
-                wide = wide + lax.dot_general(
-                    e, hot, (((1,), (1,)), ((), ())), preferred_element_type=jnp.float32
+                pos = jnp.where(wanted, f[base + 3 : base + 4, :].astype(jnp.int32), -1)
+                hot = (ids_m == pos).astype(jnp.bfloat16)
+                select[origin, b, t * most : (t + 1) * most, :] = hot[:most, :]
+                found.append(
+                    lax.dot_general(
+                        e, hot, (((1,), (1,)), ((), ())), preferred_element_type=jnp.float32
+                    )
                 )
-            step = wide[5:6, :].astype(jnp.int32) - mine
-            step = jnp.where(step < 0, step + groups, step)
-            label = wide[base : base + 1, :] + 256.0 * wide[base + 1 : base + 2, :]
-            cell = jnp.where(wide[0:1, :] > 0.5, step * owned + label.astype(jnp.int32), -1)
-            packed = wide.astype(jnp.bfloat16)
             for g in range(groups):
-                hot = (ids_c == cell - g * owned).astype(jnp.bfloat16)
-                place_in[t, q, g * owned : (g + 1) * owned, core_of * slots : (core_of + 1) * slots] = hot
+                pair = jnp.zeros((META_ROWS, slots), jnp.float32)
+                for b in range(local):
+                    pair = pair + jnp.where(rel[b] == turns + g * CAP, found[b], 0.0)
+                label = pair[base : base + 1, :] + 256.0 * pair[base + 1 : base + 2, :]
+                cell = jnp.where(pair[0:1, :] > 0.5, label.astype(jnp.int32), -1)
+                hot = (ids_c == cell).astype(jnp.bfloat16)
+                part = slice(core_of * slots, (core_of + 1) * slots)
+                place_in[t, q, g * owned : (g + 1) * owned, part] = hot
                 ext[g, t] += lax.dot_general(
-                    packed, hot, (((1,), (1,)), ((), ())), preferred_element_type=jnp.float32
+                    pair.astype(jnp.bfloat16), hot, (((1,), (1,)), ((), ())),
+                    preferred_element_type=jnp.float32,
                 )
 
     def meta_step(k, carry):
@@ -579,6 +688,7 @@
         return carry
 
     lax.fori_loop(0, chips, meta_step, 0)
+    late_start()
 
     def ext_to(step):
         return remote(
@@ -602,42 +712,211 @@
 
     def swap(c, step):
         return remote(
-            send.at[c, step - 1], recv.at[c, step - 1], swap_send.at[c, step - 1],
+            send.at[c % 2, step - 1], recv.at[c, step - 1], swap_send.at[c, step - 1],
             swap_recv.at[c, step - 1], peer(step),
         )
 
     tile = owned
 
-    def tally(c, q, first):
+    def gather_slots(c, q):
         for core_of in range(2):
             origin = q * 2 + core_of
+            got = []
             for b in range(local):
-                got = jnp.dot(
-                    select[origin, b], rows[c, origin, b], preferred_element_type=jnp.float32
-                ).astype(jnp.bfloat16)
-                for t in range(iters):
-                    compact[t, core_of * slots + b * most : core_of * slots + (b + 1) * most, :] = got[
-                        t * most : (t + 1) * most, :
-                    ]
+                x = jnp.dot(select[origin, b], rows[c, origin, b], preferred_element_type=jnp.float32)
+                got.append(x.astype(jnp.bfloat16).reshape(iters * most // 16, 16, width))
+            for g in range(groups):
+                for i in range(CAP):
+                    put = got[0] * share[origin, 0, g * CAP + i][None]
+                    for b in range(1, local):
+                        put = put + got[b] * share[origin, b, g * CAP + i][None]
+                    put = put.reshape(iters, most, width)
+                    at = core_of * slots + i * most
+                    for t in range(iters):
+                        compact[t, g, at : at + most, :] = put[t]
+
+    def tally(c, q):
+        gather_slots(c, q)
 
         def body(i, carry):
             for t in range(iters):
                 part = pl.ds(pl.multiple_of(i * tile, tile), tile)
                 acc[t, part, :] += jnp.dot(
-                    place_in[t, q, part, :], compact[t], preferred_element_type=jnp.float32
+                    place_in[t, q, part, :], compact[t, i], preferred_element_type=jnp.float32
                 )
             return carry
 
         lax.fori_loop(0, groups, body, 0)
+
+    def decode(word):
+        high = lax.shift_right_logical(word, 16)
+        low = word & 0xFFFF
+        return [high.astype(jnp.float32) - HALF, low.astype(jnp.float32) - HALF]
+
+    def late_codes(x, kind):
+        to = mate if kind == 2 else chips - 1 - chip
+        slot = 0 if kind == 2 else kind
+        device = (mine, to * 2 + core)
+        return (
+            remote(late_out.at[x, kind], late_in.at[x, slot], code_s.at[x, kind], code_r.at[x, slot], device),
+            remote(
+                late_scale_out.at[x, kind], late_scale_in.at[x, slot], scale_s.at[x, kind],
+                scale_r.at[x, slot], device,
+            ),
+        )
+
+    ones = jnp.ones((LANES, LANES), jnp.bfloat16)
+
+    def late_emit(x, kind, sums_of):
+        for i in range(reps):
+            part = slice(i * LANES, (i + 1) * LANES)
+            codes = []
+            for t, value in enumerate(sums_of(part)):
+                power = (value * value * 1.02).astype(jnp.bfloat16)
+                tall_norm = jnp.dot(power, ones, preferred_element_type=jnp.float32)
+                wide_norm = lax.dot_general(
+                    ones[:16], power, (((1,), (1,)), ((), ())), preferred_element_type=jnp.float32
+                )
+                late_scale_out[x, kind, t : t + 1, part] = (
+                    jnp.sqrt(jnp.maximum(wide_norm[0:1], 1e-30)) * (1.0 / LEVELS)
+                )
+                inverse = LEVELS * lax.rsqrt(jnp.maximum(tall_norm, 1e-30))
+                codes.append((value * inverse + (HALF + 0.5)).astype(jnp.int32))
+            late_out[x, kind, part, :] = (codes[0] << 16) | codes[1]
+        for copy in late_codes(x, kind):
+            copy.start()
+
+    def late_wait(x, slot):
+        for copy in (
+            remote(late_out.at[x, slot], late_in.at[x, slot], code_s.at[x, slot], code_r.at[x, slot], partner),
+            remote(
+                late_scale_out.at[x, slot], late_scale_in.at[x, slot], scale_s.at[x, slot],
+                scale_r.at[x, slot], partner,
+            ),
+        ):
+            copy.wait_recv()
+
+    def late_sums(x, target, slot, part):
+        values = decode(late_in[x, slot, part, :])
+        return [
+            late_acc[x, target, t, part, :] + v * tall(late_scale_in[x, slot, t : t + 1, part])
+            for t, v in enumerate(values)
+        ]
+
+    ids_w = lax.broadcasted_iota(jnp.int32, (owned, groups * slots), 0)
+
+    def late_tally(target, wanted_range, at):
+        for t in range(iters):
+            base = FIXED + 4 * t
+            for g in range(groups):
+                found = []
+                for i in range(CAP):
+                    e = late_metas[at, g, i]
+                    f = e.astype(jnp.float32)
+                    wanted = (f[base + 2 : base + 3, :].astype(jnp.int32) == wanted_range) & (f[0:1, :] > 0.5)
+                    pos = jnp.where(wanted, f[base + 3 : base + 4, :].astype(jnp.int32), -1)
+                    hot = (ids_m == pos).astype(jnp.bfloat16)
+                    late_select[g, i, t * most : (t + 1) * most, :] = hot[:most, :]
+                    x = lax.dot_general(
+                        e, hot, (((1,), (1,)), ((), ())), preferred_element_type=jnp.float32
+                    )
+                    found.append(jnp.where(turns == i, x, 0.0))
+                pair = found[0]
+                for x in found[1:]:
+                    pair = pair + x
+                label = pair[base : base + 1, :] + 256.0 * pair[base + 1 : base + 2, :]
+                late_cells[t, :, g * slots : (g + 1) * slots] = jnp.where(
+                    pair[0:1, :] > 0.5, label.astype(jnp.int32), -1
+                )
+        for x in range(late):
+            for g in range(groups):
+                for i in range(CAP):
+                    got = jnp.dot(
+                        late_select[g, i], late_rows[x, at, g, i], preferred_element_type=jnp.float32
+                    ).astype(jnp.bfloat16)
+                    spot = g * slots + i * most
+                    for t in range(iters):
+                        late_compact[x, t, spot : spot + most, :] = got[t * most : (t + 1) * most, :]
+        for t in range(iters):
+            hot = (ids_w == late_cells[t]).astype(jnp.bfloat16)
+            for x in range(late):
+                late_acc[x, target, t] += jnp.dot(
+                    hot, late_compact[x, t], preferred_element_type=jnp.float32
+                )
+
+    def late_step(j):
+        order = (j % 8) // 2
+        target = jnp.where(order == 2, 0, jnp.where(order == 3, 3, order + 1))
+        at = (j // 8) * 2 + j % 2
+        wanted_range = targets[0]
+        for i in range(1, 4):
+            wanted_range = jnp.where(target == i, targets[i], wanted_range)
+
+        @pl.when(j == 0)
+        def _():
+            for x in range(late + 1):
+                late_partner(x).wait_recv()
+
+        @pl.when((j == 8) & jnp.logical_not(is_end))
+        def _():
+            for x in range(late + 1):
+                late_inward(x).wait_recv()
+                late_share(x).start()
+            for x in range(late + 1):
+                late_share(x).wait_recv()
+
+        here = jnp.where(is_end, (target == 0) & (at < 2), (target != 3) | (at < 2))
+
+        @pl.when(here & (j < 16))
+        def _():
+            late_tally(target, wanted_range, at)
+
+        for kind, when in ((0, 9), (1, 11)):
+
+            @pl.when((j == when) & jnp.logical_not(is_end))
+            def _():
+                for x in range(late):
+                    late_emit(
+                        x, kind, lambda part: [late_acc[x, kind + 1, t, part, :] for t in range(iters)]
+                    )
+
+        @pl.when((j == 15) & jnp.logical_not(is_end))
+        def _():
+            for x in range(late):
+                late_wait(x, 1)
+                late_emit(x, 2, lambda part: late_sums(x, 3, 1, part))
+
+    def finish_late(x):
+        load_prior(chunks + x).wait()
+        late_wait(x, 0)
+        for i in range(reps):
+            part = slice(i * LANES, (i + 1) * LANES)
+            update(chunks + x, part, late_sums(x, 0, 0, part))
+
+    def update(c, part, sums):
+        previous = prior[c, part, :]
+        for t in range(iters):
+            count = cnt[t, part, :]
+            if t == iters - 1:
+                within[part, :] += previous * (count * previous - 2.0 * sums[t])
+            previous = (sums[t] + PRIOR * previous) / (count + PRIOR)
+        at = c * width
+        out[part, pl.ds(at if isinstance(at, int) else pl.multiple_of(at, width), width)] = previous
 
     def settle(c):
         for t in range(iters):
             own[c, t] = acc[t, :owned, :]
+
+        @pl.when(c >= 2)
+        def _():
+            for step in range(1, groups):
+                swap(c - 2, step).wait_send()
+
         for step in range(1, groups):
             part = slice(step * owned, (step + 1) * owned)
             high = (acc[0, part, :] * inv[step - 1, 0] + (HALF + 0.5)).astype(jnp.int32)
             low = (acc[1, part, :] * inv[step - 1, 1] + (HALF + 0.5)).astype(jnp.int32)
-            send[c, step - 1] = (high << 16) | low
+            send[c % 2, step - 1] = (high << 16) | low
             swap(c, step).start()
         acc[...] = jnp.zeros_like(acc)
 
@@ -662,18 +941,9 @@
             part = slice(i * LANES, (i + 1) * LANES)
             sums = [own[c, t, part, :] for t in range(iters)]
             for step in range(1, groups):
-                word = recv[c, step - 1, part, :]
-                high = lax.shift_right_logical(word, 16)
-                low = word & 0xFFFF
-                for t, code in enumerate((high, low)):
-                    sums[t] = sums[t] + (code.astype(jnp.float32) - HALF) * scale[step - 1, t, part, :]
-            previous = prior[c, part, :]
-            for t in range(iters):
-                count = cnt[t, part, :]
-                if t == iters - 1:
-                    within[part, :] += previous * (count * previous - 2.0 * sums[t])
-                previous = (sums[t] + PRIOR * previous) / (count + PRIOR)
-            out[part, pl.ds(pl.multiple_of(c * width, width), width)] = previous
+                for t, value in enumerate(decode(recv[c, step - 1, part, :])):
+                    sums[t] = sums[t] + value * scale[step - 1, t, part, :]
+            update(c, part, sums)
 
     def main_step(j, carry):
         c, k = j // chips, j % chips
@@ -685,7 +955,8 @@
             pull(ahead)
 
         from_partner(c, q).wait_recv()
-        tally(c, q, k == 0)
+        tally(c, q)
+        late_step(j)
 
         @pl.when(k == chips - 1)
         def _():
@@ -702,6 +973,8 @@
         return carry
 
     lax.fori_loop(0, chunks * chips, main_step, 0)
+    for x in range(late):
+        finish_late(x)
     finish(chunks - 1)
 
     for i in range(reps):
@@ -738,7 +1011,29 @@
         return carry
 
     lax.fori_loop(0, chunks * chips, drain, 0)
-    for c in range(chunks):
+
+    for x in range(late + 1):
+        for step in range(1, groups):
+            late_swap(x, step).wait_send()
+        late_partner(x).wait_send()
+
+        @pl.when(is_end)
+        def _():
+            late_inward(x).wait_send()
+
+        @pl.when(jnp.logical_not(is_end))
+        def _():
+            late_share(x).wait_send()
+
+    for x in range(late):
+
+        @pl.when(jnp.logical_not(is_end))
+        def _():
+            for kind in range(3):
+                for copy in late_codes(x, kind):
+                    copy.wait_send()
+
+    for c in range(chunks - 2, chunks):
         for step in range(1, groups):
             swap(c, step).wait_send()
 
@@ -746,8 +1041,9 @@
 def fused_buffers(local, block_rows, features, iters, owned, groups, shards):
     chips = shards // 2
     most = 2 * block_rows // shards
-    width, chunks = LANES, features // LANES
-    slots = local * most
+    width, late = LANES, features // LANES // 3
+    chunks = features // LANES - late
+    slots = CAP * most
     vmem = pltpu.VMEM
     f32, b16, i32 = jnp.float32, jnp.bfloat16, jnp.int32
     buffers = [
@@ -756,35 +1052,53 @@
         ((shards, local, iters * most, block_rows), b16),
         ((iters, chips, groups * owned, 2 * slots), b16),
         ((iters, groups * owned, width), f32),
-        ((iters, 2 * slots, width), b16),
+        ((iters, groups, 2 * slots, width), b16),
         ((chunks, iters, owned, width), f32),
-        ((chunks, groups - 1, owned, width), i32),
+        ((2, groups - 1, owned, width), i32),
         ((chunks, groups - 1, owned, width), i32),
         ((groups - 1, iters, owned, width), f32),
         ((groups - 1, iters, owned, width), f32),
         ((iters, owned, width), f32),
         ((groups, iters, META_ROWS, owned), f32),
         ((groups - 1, iters, META_ROWS, owned), f32),
-        ((chunks, owned, width), f32),
+        ((chunks + late, owned, width), f32),
         ((owned, width), f32),
         ((META_ROWS, block_rows), f32),
+        ((shards, local, groups * CAP, 16, LANES), b16),
+        ((late, local, block_rows, width), b16),
+        ((late, groups - 1, CAP, block_rows, width), b16),
+        ((late, 4, groups, CAP, block_rows, width), b16),
+        ((groups - 1, CAP, META_ROWS, block_rows), b16),
+        ((4, groups, CAP, META_ROWS, block_rows), b16),
+        ((groups, CAP, iters * most, block_rows), b16),
+        ((iters, 1, groups * slots), i32),
+        ((late, iters, groups * slots, width), b16),
+        ((late, 4, iters, owned, width), f32),
+        ((late, 3, owned, width), i32),
+        ((late, 2, owned, width), i32),
+        ((late, 3, 8, owned), f32),
+        ((late, 2, 8, owned), f32),
     ]
     dma = pltpu.SemaphoreType.DMA
-    sems = [dma((chunks,)), dma((chunks,))]
+    sems = [dma((chunks,)), dma((chunks + late,))]
     sems += [dma((chips,))] * 4
     sems += [dma((chunks, chips))] * 6
     sems += [dma((groups - 1,))] * 2
     sems += [dma((chunks, groups - 1))] * 2
-    return [vmem(s, d) for s, d in buffers], sems, buffers, most, chunks
+    sems += [dma((late,))] + [dma((late + 1, groups - 1))] * 2 + [dma((late + 1,))] * 6
+    sems += [dma((late, 3)), dma((late, 2))] * 2
+    return [vmem(s, d) for s, d in buffers], sems, buffers, most, chunks, late
 
 
 def fits(local, block_rows, features, iters, owned, groups, shards):
     if features % LANES or features < 2 * LANES or owned % LANES or shards % 2:
+        return False
+    if shards != 8 or features < 6 * LANES:
         return False
     if iters != 2 or 4 * iters + FIXED > META_ROWS or (2 * block_rows) % shards:
         return False
     most = 2 * block_rows // shards
-    if (local * most) % LANES or most % 16 or block_rows % LANES:
+    if (CAP * most) % LANES or CAP * most > block_rows or most % 16 or block_rows % LANES:
         return False
     total = 0
     for shape, dtype in fused_buffers(local, block_rows, features, iters, owned, groups, shards)[2]:
@@ -792,7 +1106,7 @@
         for extent in shape:
             size *= extent
         total += size
-    return total < 58 * 2**20
+    return total < 60 * 2**20
 
 
 def fused_body(embeddings, assignments, block_group, centroids):
@@ -800,12 +1114,12 @@
     local, block_rows, features = embeddings.shape
     iters = assignments.shape[1]
     owned = centroids.shape[1] // shards
-    buffers, sems, unused, most, chunks = fused_buffers(
+    buffers, sems, unused, most, chunks, late = fused_buffers(
         local, block_rows, features, iters, owned, groups, shards
     )
 
     out, inertia = pl.pallas_call(
-        functools.partial(fused_kernel, chunks, most),
+        functools.partial(fused_kernel, chunks, late, most),
         out_shape=[
             pltpu.VMEM((owned, features), jnp.float32),
             pltpu.VMEM((1, owned), jnp.float32),
@@ -819,7 +1133,7 @@
         out_specs=[pl.BlockSpec(memory_space=pltpu.VMEM)] * 2,
         scratch_shapes=buffers + sems,
         compiler_params=pltpu.CompilerParams(
-            collective_id=0, has_side_effects=True, vmem_limit_bytes=56 * 2**20
+            collective_id=0, has_side_effects=True, vmem_limit_bytes=61 * 2**20
         ),
     )(block_group, assignments, embeddings, centroids)
     return out[None], inertia

time: 139 us -> 128 us (0.921)
  Pallas kernels: 137 us -> 125 us
    pallas_call x1, Pallas kernels: 137 us -> 125 us  [fused_body(): pl.pallas_call(functools.partial(fused_kernel, chunks, late, most), out_s...]
where the time goes in v3:
time: 128 us
  Pallas kernels  125 us (98%)
  local copies, waits for them, and re-layouts  1.72 us (1%)
    pallas_call x1, Pallas kernels, fused_body(): pl.pallas_call(functools.partial(fused_kernel, chunks, late, most), out_s...  125 us

profile of v3, /device:TPU:0, one launch (start us, length us, event | category | flops | bytes accessed | tf_op | source)
XLA Modules:
  0.0 127.6 jit_solution(9273632965416231501)
XLA Ops:
  0.6 125.3 %shard_map.59 = (f32[512,768]{1,0:T(8,128)S(1)}, f32[1,512]{1,0:T(1,128)S(1)}) custom-call(s32[4]{0:T(128)} %owner_in.1, s32[4,2,256]{2,1,0:T(2,128)} %label_in.1, bf16[4,256,768]{2,1,0:T(8,128)(2,1)} %emb.1, f32[1,4096,768]{2,1,0:T(8,128)} %cents.1), custom_call_target="tpu_custom_call" | custom-call | tf_op jit(solution)/shard_map/pallas_call | solution.py:1121
  125.9 1.1 copy.8
  127.0 0.6 copy.9

commit v4 on v3

--- a/solution.py
+++ b/solution.py
@@ -509,6 +509,11 @@
         meta_to(other).start()
     issue_own(1)
 
+    @pl.when(is_end)
+    def _():
+        for c in range(2, chunks):
+            issue_own(c)
+
     def late_swap(x, step):
         sent = late_meta_send if x == late else late_send.at[x]
         kept = late_metas if x == late else late_rows.at[x]
@@ -594,7 +599,7 @@
         c, k = j // chips, j % chips
         q = source(k)
 
-        @pl.when((k == 0) & (c + 2 < chunks))
+        @pl.when((k == 0) & (c + 2 < chunks) & jnp.logical_not(is_end))
         def _():
             issue_own(c + 2)
 
@@ -685,6 +690,11 @@
         for core_of in range(2):
             take_meta(q, core_of)
         pull(k)
+
+        @pl.when((both > 0) & (k >= chips - 2))
+        def _():
+            pull(k + 2)
+
         return carry
 
     lax.fori_loop(0, chips, meta_step, 0)
@@ -846,7 +856,7 @@
 
     def late_step(j):
         order = (j % 8) // 2
-        target = jnp.where(order == 2, 0, jnp.where(order == 3, 3, order + 1))
+        target = jnp.where(order == 2, 0, jnp.where(order == 3, 3, 2 - order))
         at = (j // 8) * 2 + j % 2
         wanted_range = targets[0]
         for i in range(1, 4):
@@ -871,7 +881,7 @@
         def _():
             late_tally(target, wanted_range, at)
 
-        for kind, when in ((0, 9), (1, 11)):
+        for kind, when in ((1, 9), (0, 11)):
 
             @pl.when((j == when) & jnp.logical_not(is_end))
             def _():
@@ -880,7 +890,7 @@
                         x, kind, lambda part: [late_acc[x, kind + 1, t, part, :] for t in range(iters)]
                     )
 
-        @pl.when((j == 15) & jnp.logical_not(is_end))
+        @pl.when((j == 14) & jnp.logical_not(is_end))
         def _():
             for x in range(late):
                 late_wait(x, 1)
@@ -948,9 +958,9 @@
     def main_step(j, carry):
         c, k = j // chips, j % chips
         q = source(k)
-        ahead = j + jnp.where(both > 0, chips, 0)
-
-        @pl.when((ahead >= chips) & (ahead < chunks * chips))
+        ahead = j + jnp.where(both > 0, chips + 2, 0)
+
+        @pl.when((ahead >= jnp.where(both > 0, chips + 2, chips)) & (ahead < chunks * chips))
         def _():
             pull(ahead)
 

time: 128 us -> 113 us (0.88)
  Pallas kernels: 125 us -> 109 us
    pallas_call x1, Pallas kernels: 125 us -> 109 us  [fused_body(): pl.pallas_call(functools.partial(fused_kernel, chunks, late, most), out_s...]
where the time goes in v4:
time: 113 us; the launch traced here: 111 us
  Pallas kernels  109 us (96%)
  local copies, waits for them, and re-layouts  1.72 us (2%)
    pallas_call x1, Pallas kernels, fused_body(): pl.pallas_call(functools.partial(fused_kernel, chunks, late, most), out_s...  109 us

profile of v4, /device:TPU:0, one launch (start us, length us, event | category | flops | bytes accessed | tf_op | source)
XLA Modules:
  0.0 111.4 jit_solution(9447920471970219810)
XLA Ops:
  0.6 109.1 %shard_map.59 = (f32[512,768]{1,0:T(8,128)S(1)}, f32[1,512]{1,0:T(1,128)S(1)}) custom-call(s32[4]{0:T(128)} %owner_in.1, s32[4,2,256]{2,1,0:T(2,128)} %label_in.1, bf16[4,256,768]{2,1,0:T(8,128)(2,1)} %emb.1, f32[1,4096,768]{2,1,0:T(8,128)} %cents.1), custom_call_target="tpu_custom_call" | custom-call | tf_op jit(solution)/shard_map/pallas_call | solution.py:1131
  109.7 1.1 %copy.8 = f32[1,512,768]{2,1,0:T(8,128)} copy(f32[1,512,768]{2,1,0:T(8,128)S(1)} %bitcast.1) | data formatting | bytes 3145728
  110.9 0.6 copy.9

commit v5 on v4

--- a/solution.py
+++ b/solution.py
@@ -756,7 +756,7 @@
                 )
             return carry
 
-        lax.fori_loop(0, groups, body, 0)
+        lax.fori_loop(0, groups, body, 0, unroll=True)
 
     def decode(word):
         high = lax.shift_right_logical(word, 16)
@@ -854,14 +854,21 @@
                     hot, late_compact[x, t], preferred_element_type=jnp.float32
                 )
 
-    def late_step(j):
-        order = (j % 8) // 2
-        target = jnp.where(order == 2, 0, jnp.where(order == 3, 3, 2 - order))
-        at = (j // 8) * 2 + j % 2
+    def late_run(j, codes):
+        code_of = jnp.int32(codes[0])
+        for i, entry in enumerate(codes):
+            code_of = jnp.where(j == i, entry, code_of)
+        target, at = code_of // 4, code_of % 4
         wanted_range = targets[0]
         for i in range(1, 4):
             wanted_range = jnp.where(target == i, targets[i], wanted_range)
-
+        here = jnp.where(is_end, (target == 0) & (at < 2), True)
+
+        @pl.when(here & (j < len(codes)))
+        def _():
+            late_tally(target, wanted_range, at)
+
+    def late_step(j):
         @pl.when(j == 0)
         def _():
             for x in range(late + 1):
@@ -875,11 +882,7 @@
             for x in range(late + 1):
                 late_share(x).wait_recv()
 
-        here = jnp.where(is_end, (target == 0) & (at < 2), (target != 3) | (at < 2))
-
-        @pl.when(here & (j < 16))
-        def _():
-            late_tally(target, wanted_range, at)
+        late_run(j, (8, 9, 4, 5, 12, 13, 0, 1, 10, 11, 6, 7))
 
         for kind, when in ((1, 9), (0, 11)):
 
@@ -972,17 +975,18 @@
         def _():
             settle(c)
 
-            @pl.when(c == 0)
-            def _():
-                scales()
-
-            @pl.when(c > 0)
-            def _():
-                finish(c - 1)
 
         return carry
 
     lax.fori_loop(0, chunks * chips, main_step, 0)
+    def late_rest(j, carry):
+        late_run(j, (2, 3))
+        return carry
+
+    lax.fori_loop(0, 2, late_rest, 0)
+    scales()
+    for c in range(chunks - 1):
+        finish(c)
     for x in range(late):
         finish_late(x)
     finish(chunks - 1)

time: 113 us -> 107 us (0.947)
  the two profiles are of different devices: /device:TPU:0 before, /device:TPU:9 now
where the time goes in v5:
time: 107 us
  Pallas kernels  105 us (98%)
  local copies, waits for them, and re-layouts  1.72 us (2%)
    pallas_call x1, Pallas kernels, fused_body(): pl.pallas_call(functools.partial(fused_kernel, chunks, late, most), out_s...  105 us

profile of v5, /device:TPU:9, one launch (start us, length us, event | category | flops | bytes accessed | tf_op | source)
XLA Modules:
  0.0 107.1 jit_solution(13993823448161306439)
XLA Ops:
  0.6 104.7 %shard_map.59 = (f32[512,768]{1,0:T(8,128)S(1)}, f32[1,512]{1,0:T(1,128)S(1)}) custom-call(s32[4]{0:T(128)} %owner_in.1, s32[4,2,256]{2,1,0:T(2,128)} %label_in.1, bf16[4,256,768]{2,1,0:T(8,128)(2,1)} %emb.1, f32[1,4096,768]{2,1,0:T(8,128)} %cents.1), custom_call_target="tpu_custom_call" | custom-call | tf_op jit(solution)/shard_map/pallas_call | solution.py:1135
  105.3 1.1 %copy.8 = f32[1,512,768]{2,1,0:T(8,128)} copy(f32[1,512,768]{2,1,0:T(8,128)S(1)} %bitcast.1) | data formatting | bytes 3145728
  106.5 0.6 copy.9
